TPU v7x, 32 devices: a whole 2x2x4 slice. The times are simulated.
32 devices in a mesh: blk: 8 (over z, x), grp: 4 (over y, core).
Axes of the slice: x: 2, y: 2, z: 4, core: 2. Of those that a mesh axis runs over, the one named last changes fastest.
Arguments:
- positions: float32 [3, 2048], P(None, ('blk', 'grp')), may hold values from -0.25 to 31.25, as said below
- moments: float32 [2, 2, 3, 2048], P(None, None, None, ('blk', 'grp')), may hold values from -6 to 6
- inv_polar_re: float32 [2048], P(('blk', 'grp')), may hold values from 0.5 to 2
- inv_polar_im: float32 [2048], P(('blk', 'grp')), may hold values from -0.5 to 0.5
- mode_field: float32 [2, 3, 2048, 512], P(None, None, ('blk', 'grp')), may hold values from -0.078125 to 0.078125
- mode_detune: float32 [512], replicated, may hold values from -1 to 1
- mode_width: float32 [512], replicated, may hold values from 0.05 to 1
Outputs:
- response: float32 [2, 2, 3, 2048], P(None, None, None, ('blk', 'grp'))
Inputs may be any that keep to these rules, and one draw needn't show every extreme that they name: `positions`: dipole n lies within 0.25, in each coordinate, of the lattice site (n % 32, (n // 32) % 32, n // 1024); distinct dipoles are at least 0.5 apart.
All inputs are finite; a program needn't handle non-finite values.
Results may differ from a plain program's by a relative error of at most 0.0003.
Values sent between devices are 32-bit elements; how exact they have to be, the bound alone decides.
No kernel may reach another device: no remote copies, remote signals or barrier semaphores. Data moves between devices by JAX's collectives and lax.ppermute only.
A program may use at most 64 MiB of HBM per device.

v0:
```python
import math
import jax
import jax.numpy as jnp
from jax import lax
from jax.sharding import PartitionSpec as P

wavenumber = 1.0
coupling = 0.05
near_limit = 0.04


def pair_field(deltas, dipoles, axis_sum):
    delta_x, delta_y, delta_z = deltas
    square = delta_x * delta_x + delta_y * delta_y + delta_z * delta_z
    coincide = square < near_limit
    safe_square = jnp.where(coincide, 1.0, square)
    inverse = 1.0 / jnp.sqrt(safe_square)
    phase_arg = wavenumber * safe_square * inverse
    cos_val = jnp.cos(phase_arg)
    sine_val = jnp.sin(phase_arg)
    masked_cube = jnp.where(coincide, 0.0, inverse * inverse * inverse)
    near_re = phase_arg * phase_arg - 1.0
    far_re = 3.0 - phase_arg * phase_arg
    diag_re = (cos_val * near_re - sine_val * phase_arg) * masked_cube
    diag_im = (sine_val * near_re + cos_val * phase_arg) * masked_cube
    scaled = masked_cube / safe_square
    outer_re = (cos_val * far_re + 3.0 * sine_val * phase_arg) * scaled
    outer_im = (sine_val * far_re - 3.0 * cos_val * phase_arg) * scaled
    tile_list = []
    for drive_set in range(len(dipoles) // 6):
        moment_re = dipoles[6 * drive_set : 6 * drive_set + 3]
        moment_im = dipoles[6 * drive_set + 3 : 6 * drive_set + 6]
        proj_re = delta_x * moment_re[0] + delta_y * moment_re[1] + delta_z * moment_re[2]
        proj_im = delta_x * moment_im[0] + delta_y * moment_im[1] + delta_z * moment_im[2]
        along_re = outer_re * proj_re - outer_im * proj_im
        along_im = outer_re * proj_im + outer_im * proj_re
        for component in range(3):
            tile_list.append(
                diag_re * moment_re[component]
                - diag_im * moment_im[component]
                + deltas[component] * along_re
            )
        for component in range(3):
            tile_list.append(
                diag_re * moment_im[component]
                + diag_im * moment_re[component]
                + deltas[component] * along_im
            )
    return jnp.stack([jnp.sum(entry_tile, axis=axis_sum) for entry_tile in tile_list])


def contract(left, right):
    return lax.dot_general(left, right, (((0,), (1,)), ((), ())), precision=lax.Precision.HIGHEST)


def modal_project(mode_rows, moment_rows):
    amp_re = contract(mode_rows[0], moment_rows[:, 0]) - contract(mode_rows[1], moment_rows[:, 1])
    amp_im = contract(mode_rows[0], moment_rows[:, 1]) + contract(mode_rows[1], moment_rows[:, 0])
    return (amp_re, amp_im)


def spread(weights, rows):
    return lax.dot_general(weights, rows, (((0,), (1,)), ((), ())), precision=lax.Precision.HIGHEST)


def modal_spread(mode_rows, amp_re, amp_im, mode_detune, mode_width):
    denominator = mode_detune * mode_detune + mode_width * mode_width
    resp_re = (mode_detune / denominator)[:, None]
    resp_im = (mode_width / denominator)[:, None]
    weighted_re = resp_re * amp_re - resp_im * amp_im
    weighted_im = resp_re * amp_im + resp_im * amp_re
    out_re = spread(weighted_re, mode_rows[0]) - spread(weighted_im, mode_rows[1])
    out_im = spread(weighted_re, mode_rows[1]) + spread(weighted_im, mode_rows[0])
    return jnp.stack([out_re, out_im], axis=1)


def combine(moments, inv_polar_re, inv_polar_im, pair_part, modal_part):
    drives = moments.shape[0]
    dipole_count = moments.shape[3]
    field_sum = coupling * pair_part.reshape(drives, 2, 3, dipole_count) + modal_part.reshape(
        drives, 2, 3, dipole_count
    )
    moment_re = moments[:, 0]
    moment_im = moments[:, 1]
    resp_re = inv_polar_re * moment_re - inv_polar_im * moment_im - field_sum[:, 0]
    resp_im = inv_polar_re * moment_im + inv_polar_im * moment_re - field_sum[:, 1]
    return jnp.stack([resp_re, resp_im], axis=1)


def on_device(positions, moments, inv_polar_re, inv_polar_im, mode_field, mode_detune, mode_width):
    drives = moments.shape[0]
    dipole_count = positions.shape[1]
    flat_moments = moments.reshape(drives * 6, dipole_count)
    mode_rows = mode_field.reshape(2, 3 * dipole_count, mode_field.shape[3])
    amp_re, amp_im = modal_project(mode_rows, moments.reshape(drives, 2, 3 * dipole_count))
    amp_re, amp_im = lax.psum((amp_re, amp_im), ("blk", "grp"))
    modal_part = modal_spread(mode_rows, amp_re, amp_im, mode_detune, mode_width).reshape(
        drives * 6, dipole_count
    )
    group_pos, group_moments = (
        lax.all_gather(positions, "grp", axis=1, tiled=True),
        lax.all_gather(flat_moments, "grp", axis=1, tiled=True),
    )
    initial = jnp.zeros((drives * 6, dipole_count), jnp.float32)
    places = lax.all_gather(group_pos, "blk", axis=1, tiled=True)
    dipoles = lax.all_gather(group_moments, "blk", axis=1, tiled=True)
    columns = places.shape[1]
    block_width = math.gcd(columns, 2048)

    def advance(block, inner):
        source_pos = lax.dynamic_slice_in_dim(places, block * block_width, block_width, 1)
        source_mom = lax.dynamic_slice_in_dim(dipoles, block * block_width, block_width, 1)
        deltas = [positions[axis_c][:, None] - source_pos[axis_c][None, :] for axis_c in range(3)]
        return inner + pair_field(
            deltas, [source_mom[member][None, :] for member in range(drives * 6)], 1
        )

    pair_part = lax.fori_loop(0, columns // block_width, advance, initial)
    return combine(moments, inv_polar_re, inv_polar_im, pair_part, modal_part)


def solution(mesh):
    placed = (
        P(None, ("blk", "grp")),
        P(None, None, None, ("blk", "grp")),
        P(("blk", "grp")),
        P(("blk", "grp")),
        P(None, None, ("blk", "grp"), None),
        P(),
        P(),
    )
    return jax.shard_map(
        on_device,
        mesh=mesh,
        in_specs=placed,
        out_specs=P(None, None, None, ("blk", "grp")),
        check_vma=False,
    )
```

profile of v0, /device:TPU:0, one launch (start us, length us, event | category | flops | bytes accessed | tf_op | source)
XLA Modules:
  0.0 126.5 jit_solution(16070612129556951673)
XLA Ops:
  0.0 0.0 copy-start.1
  0.0 1.2 fusion.63
  1.2 0.0 copy-done.1
  1.2 0.1 reshape.26
  1.3 0.3 fusion.53
  1.6 0.3 convolution_subtract_fusion
  1.9 0.3 fusion.49
  2.3 0.3 convolution_add_fusion
  2.6 42.1 %all-reduce = (f32[512,2]{0,1:T(2,128)S(1)}, f32[512,2]{0,1:T(2,128)S(1)}) all-reduce(f32[512,2]{0,1:T(2,128)S(1)} %convolution_add_fusion, f32[512,2]{0,1:T(2,128)S(1)} %convolution_subtract_fusion), channel_id=1, replica_groups=mesh['blk'=8,'grp'=4] {'blk','grp'}, use_global_device_ids=true, to_apply=%region_13.0 | all-reduce | flops 2048 | bytes 16384 | tf_op jit(solution)/shard_map/psum | solution.py:96
  44.7 0.0 copy-done.3
  44.7 0.7 copy-done.2
  45.4 0.4 fusion.62
  45.8 0.4 convolution_subtract_fusion.1
  46.2 0.1 stack.79
  46.3 0.4 fusion.61
  46.7 0.4 convolution_add_fusion.1
  47.1 0.1 stack.80
  47.2 5.5 %all-gather.1 = f32[4,64,12]{1,2,0:T(8,128)S(1)} all-gather(f32[1,64,12]{1,2,0:T(8,128)S(1)} %bitcast.76), channel_id=1, replica_groups=mesh['blk'=8,'grp'=4] {'grp'}, dimensions={0}, use_global_device_ids=true | all-gather | bytes 15360 | tf_op jit(solution)/shard_map/all_gather | solution.py:102
  52.8 0.1 reshape.30
  52.9 30.5 %all_gather.15 = f32[12,2048]{1,0:T(8,128)S(1)} all-gather(f32[12,256]{1,0:T(8,128)S(1)} %bitcast.75), channel_id=1, replica_groups=mesh['blk'=8,'grp'=4] {'blk'}, dimensions={1}, use_global_device_ids=true | all-gather | bytes 110592 | tf_op jit(solution)/shard_map/all_gather | solution.py:106
  83.4 0.1 fusion.64
  83.4 0.0 copy-start
  83.5 0.7 copy-done
  84.1 5.2 %all-gather = f32[4,64,3]{1,2,0:T(4,128)S(1)} all-gather(f32[1,64,3]{1,2,0:T(4,128)S(1)} %bitcast.95), channel_id=1, replica_groups=mesh['blk'=8,'grp'=4] {'grp'}, dimensions={0}, use_global_device_ids=true | all-gather | bytes 3840 | tf_op jit(solution)/shard_map/all_gather | solution.py:101
  89.3 0.1 reshape.28
  89.4 30.6 %all_gather.13 = f32[3,2048]{1,0:T(4,128)S(1)} all-gather(f32[3,256]{1,0:T(4,128)S(1)} %bitcast.77), channel_id=1, replica_groups=mesh['blk'=8,'grp'=4] {'blk'}, dimensions={1}, use_global_device_ids=true | all-gather | bytes 27648 | tf_op jit(solution)/shard_map/all_gather | solution.py:105
  120.0 5.1 %fusion.45 = (f32[64]{0:T(128)S(1)}, f32[64]{0:T(128)S(1)}, f32[64]{0:T(128)S(1)}, f32[64]{0:T(128)S(1)}, f32[64]{0:T(128)S(1)}, /*index=5*/f32[64]{0:T(128)S(1)...) fusion(f32[2048]{0:T(1024)S(1)} %bitcast.81, ...), kind=kLoop, calls=%fused_computation.80 | loop fusion | flops 18349312 | bytes 126720 | tf_op jit(solution)/shard_map/while/body/eval_jaxpr/reduce_sum | solution.py:49
  125.2 0.0 copy-start.4
  125.2 0.0 copy-start.5
  125.2 0.6 copy-done.4
  125.9 0.0 copy-done.5
  125.9 0.6 copy.37
  (16 shorter events, 0.2 us)
Async XLA Ops:
  0.0 1.2 copy-start.1
  2.6 42.1 %copy-start.3 = (f32[512]{0:T(512)S(1)}, f32[512]{0:T(512)}, u32[]{:S(2)}) copy-start(f32[512]{0:T(512)} %param.13) | copy-start | bytes 6148
  44.7 0.7 copy-start.2
  83.4 0.7 copy-start
  125.2 0.7 copy-start.4
  125.2 0.7 copy-start.5
where the time goes:
time: 127 us; the launch traced here: 126 us
  blocking collectives  114 us (90%)
  other arithmetic  5.14 us (4%)
  local copies, waits for them, and re-layouts  4.42 us (3%)
  matrix products  2.95 us (2%)
    psum x1, blocking collectives, on_device(): amp_re, amp_im = lax.psum((amp_re, amp_im), ('blk', 'grp'))  42.1 us
    all_gather x1, blocking collectives, on_device(): places = lax.all_gather(group_pos, 'blk', axis=1, tiled=True)  30.6 us
    all_gather x1, blocking collectives, on_device(): dipoles = lax.all_gather(group_moments, 'blk', axis=1, tiled=True)  30.5 us
    all_gather x1, blocking collectives, on_device(): lax.all_gather(flat_moments, 'grp', axis=1, tiled=True)  5.52 us
    all_gather x1, blocking collectives, on_device(): lax.all_gather(positions, 'grp', axis=1, tiled=True)  5.18 us
    reduce_sum x1, other arithmetic, pair_field(): jnp.sum(entry_tile, axis=axis_sum)  5.11 us

commit v1 on v0

--- a/solution.py
+++ b/solution.py
@@ -102,8 +102,13 @@
         lax.all_gather(flat_moments, "grp", axis=1, tiled=True),
     )
     initial = jnp.zeros((drives * 6, dipole_count), jnp.float32)
-    places = lax.all_gather(group_pos, "blk", axis=1, tiled=True)
-    dipoles = lax.all_gather(group_moments, "blk", axis=1, tiled=True)
+    places, dipoles = jnp.split(
+        lax.all_gather(
+            jnp.concatenate([group_pos, group_moments], axis=0), "blk", axis=1, tiled=True
+        ),
+        [group_pos.shape[0]],
+        axis=0,
+    )
     columns = places.shape[1]
     block_width = math.gcd(columns, 2048)
 

time: 127 us -> 96.5 us (0.76)
  blocking collectives: 114 us -> 83.5 us
    all_gather x2 -> x1, blocking collectives: 61.1 us -> 30.5 us  [on_device(): lax.all_gather(jnp.concatenate([group_pos, group_moments], axis=0), 'blk'...]
where the time goes in v1:
time: 96.5 us; the launch traced here: 96.1 us
  blocking collectives  83.5 us (87%)
  other arithmetic  5.15 us (5%)
  local copies, waits for them, and re-layouts  4.42 us (5%)
  matrix products  2.95 us (3%)
    psum x1, blocking collectives, on_device(): amp_re, amp_im = lax.psum((amp_re, amp_im), ('blk', 'grp'))  42.1 us
    all_gather x1, blocking collectives, on_device(): lax.all_gather(jnp.concatenate([group_pos, group_moments], axis=0), 'blk'...  30.5 us
    all_gather x1, blocking collectives, on_device(): lax.all_gather(flat_moments, 'grp', axis=1, tiled=True)  5.52 us
    all_gather x1, blocking collectives, on_device(): lax.all_gather(positions, 'grp', axis=1, tiled=True)  5.42 us
    reduce_sum x1, other arithmetic, pair_field(): jnp.sum(entry_tile, axis=axis_sum)  5.11 us
    unnamed x15, local copies, waits for them, and re-layouts  2.18 us

profile of v1, /device:TPU:0, one launch (start us, length us, event | category | flops | bytes accessed | tf_op | source)
XLA Modules:
  0.0 96.1 jit_solution(16674815038808664368)
XLA Ops:
  0.0 0.0 copy-start.1
  0.0 1.2 %fusion.63 = (f32[1,3,64,512]{3,2,1,0:T(8,128)S(1)}, f32[1,3,64,512]{3,2,1,0:T(8,128)S(1)}) fusion(f32[2,3,64,512]{3,2,1,0:T(8,128)} %param.11), kind=kLoop, calls=%fused_computation.115 | loop fusion | bytes 1572864 | tf_op jit(solution)/shard_map/slice | solution.py:57
  1.2 0.0 copy-done.1
  1.2 0.1 reshape.26
  1.3 0.3 fusion.53
  1.6 0.3 convolution_subtract_fusion
  1.9 0.3 fusion.49
  2.3 0.3 convolution_add_fusion
  2.6 0.0 copy-start.3
  2.6 42.1 %all-reduce = (f32[512,2]{0,1:T(2,128)S(1)}, f32[512,2]{0,1:T(2,128)S(1)}) all-reduce(f32[512,2]{0,1:T(2,128)S(1)} %convolution_add_fusion, f32[512,2]{0,1:T(2,128)S(1)} %convolution_subtract_fusion), channel_id=1, replica_groups=mesh['blk'=8,'grp'=4] {'blk','grp'}, use_global_device_ids=true, to_apply=%region_13.0 | all-reduce | flops 2048 | bytes 16384 | tf_op jit(solution)/shard_map/psum | solution.py:96
  44.7 0.0 copy-start.2
  44.7 0.0 copy-done.3
  44.7 0.7 copy-done.2
  45.4 0.4 fusion.62
  45.8 0.4 convolution_subtract_fusion.1
  46.2 0.1 stack.79
  46.3 0.4 fusion.61
  46.7 0.4 convolution_add_fusion.1
  47.1 0.1 stack.80
  47.2 5.5 %all-gather.1 = f32[4,64,12]{1,2,0:T(8,128)S(1)} all-gather(f32[1,64,12]{1,2,0:T(8,128)S(1)} %bitcast.76), channel_id=1, replica_groups=mesh['blk'=8,'grp'=4] {'grp'}, dimensions={0}, use_global_device_ids=true | all-gather | bytes 15360 | tf_op jit(solution)/shard_map/all_gather | solution.py:102
  52.8 0.1 reshape.30
  52.9 0.7 copy-done
  53.5 5.4 %all-gather = f32[4,64,3]{1,2,0:T(4,128)S(1)} all-gather(f32[1,64,3]{1,2,0:T(4,128)S(1)} %bitcast.95), channel_id=1, replica_groups=mesh['blk'=8,'grp'=4] {'grp'}, dimensions={0}, use_global_device_ids=true | all-gather | bytes 3840 | tf_op jit(solution)/shard_map/all_gather | solution.py:101
  59.0 0.1 reshape.28
  59.1 30.5 %all_gather.11 = f32[15,2048]{1,0:T(8,128)S(1)} all-gather(f32[15,256]{1,0:T(8,128)S(1)} %pad_maximum_fusion), channel_id=1, replica_groups=mesh['blk'=8,'grp'=4] {'blk'}, dimensions={1}, use_global_device_ids=true | all-gather | bytes 138240 | tf_op jit(solution)/shard_map/all_gather | solution.py:106
  89.6 0.1 fusion.64
  89.7 5.1 %fusion.45 = (f32[64]{0:T(128)S(1)}, f32[64]{0:T(128)S(1)}, f32[64]{0:T(128)S(1)}, f32[64]{0:T(128)S(1)}, f32[64]{0:T(128)S(1)}, /*index=5*/f32[64]{0:T(128)S(1)...) fusion(f32[2048]{0:T(1024)S(1)} %bitcast.81, ...), kind=kLoop, calls=%fused_computation.80 | loop fusion | flops 18349312 | bytes 126720 | tf_op jit(solution)/shard_map/while/body/eval_jaxpr/reduce_sum | solution.py:49
  94.9 0.0 copy-start.4
  94.9 0.0 copy-start.5
  94.9 0.6 copy-done.4
  95.5 0.0 copy-done.5
  95.5 0.6 copy.37
  (15 shorter events, 0.1 us)
Async XLA Ops:
  0.0 1.2 %copy-start.1 = (f32[2,2,3,64]{3,1,2,0:T(2,128)S(1)}, f32[2,2,3,64]{3,1,2,0:T(2,128)}, u32[]{:S(2)}) copy-start(f32[2,2,3,64]{3,1,2,0:T(2,128)} %param.8) | copy-start | bytes 9220
  2.6 42.1 %copy-start.3 = (f32[512]{0:T(512)S(1)}, f32[512]{0:T(512)}, u32[]{:S(2)}) copy-start(f32[512]{0:T(512)} %param.13) | copy-start | bytes 6148
  44.7 0.7 copy-start.2
  52.9 0.7 copy-start
  94.9 0.7 copy-start.4
  94.9 0.7 copy-start.5
